TPU v7x, 16 devices: a 4x2x1 block of a 4x4x8 slice. The times are simulated.
16 devices in a mesh: dp: 2 (over y, z), sp: 8 (over x, core).
Axes of the slice: x: 4, y: 2, z: 1, core: 2. Of those that a mesh axis runs over, the one named last changes fastest.
The devices are a block of a 4x4x8 slice.
Arguments:
- x_patch: bfloat16 [64, 4096, 768], P('dp', 'sp'), parts along dimension 0
- w_tok1: bfloat16 [4096, 384], P('sp')
- b_tok1: float32 [384], P('sp')
- w_tok2: bfloat16 [384, 4096], P(None, 'sp')
- b_tok2: float32 [4096], P('sp')
- w_ch1: bfloat16 [768, 3072], replicated
- b_ch1: float32 [3072], replicated
- w_ch2: bfloat16 [3072, 768], replicated
- b_ch2: float32 [768], replicated
- ln1_gain: float32 [768], replicated
- ln1_bias: float32 [768], replicated
- ln2_gain: float32 [768], replicated
- ln2_bias: float32 [768], replicated
Outputs:
- output: bfloat16 [64, 4096, 768], P('dp', 'sp'), parts along dimension 0
There are 2 independent parts. A program takes and returns all parts, laid end to end along the dimension named above; an argument that names none is the same for every part.
All inputs are finite; a program needn't handle non-finite values.
Results may differ from a plain program's by a relative error of at most 0.00985338.
Values are sent between devices in bfloat16 or wider.
A program may use at most 768 MiB of HBM per device.

v0:
```python
import jax
import jax.numpy as jnp
from jax import lax
from jax.sharding import PartitionSpec as P

LN_EPS = 1e-6


def layer_norm(values, ln_gain, ln_bias):
    mean_val = jnp.mean(values, axis=-1, keepdims=True)
    centred = values - mean_val
    var_val = jnp.mean(centred * centred, axis=-1, keepdims=True)
    return centred * lax.rsqrt(var_val + LN_EPS) * ln_gain + ln_bias


def channel_mix(x_mid, w_ch1, b_ch1, w_ch2, b_ch2, ln2_gain, ln2_bias):
    mid_wide = x_mid.astype(jnp.float32)
    normed_two = layer_norm(mid_wide, ln2_gain, ln2_bias).astype(jnp.bfloat16)
    ch_pre = jnp.einsum("bsc,cf->bsf", normed_two, w_ch1, preferred_element_type=jnp.float32) + b_ch1
    ch_act = jax.nn.gelu(ch_pre).astype(jnp.bfloat16)
    ch_out = jnp.einsum("bsf,fc->bsc", ch_act, w_ch2, preferred_element_type=jnp.float32) + b_ch2
    return (mid_wide + ch_out).astype(jnp.bfloat16)


def solution(mesh):
    row_spec = P("dp", "sp", None)

    def local_layer(x_blk, w1_rows, b1_part, w2_cols, b2_part, w_ch1, b_ch1, w_ch2, b_ch2, ln1_gain, ln1_bias, ln2_gain, ln2_bias):
        x_wide = x_blk.astype(jnp.float32)
        normed = layer_norm(x_wide, ln1_gain, ln1_bias).astype(jnp.bfloat16)
        part_pre = jnp.einsum("bsc,sd->bdc", normed, w1_rows, preferred_element_type=jnp.float32)
        tok_pre = lax.psum_scatter(part_pre, "sp", scatter_dimension=1, tiled=True) + b1_part[None, :, None]
        tok_act = jax.nn.gelu(tok_pre).astype(jnp.bfloat16)
        act_full = lax.all_gather(tok_act, "sp", axis=1, tiled=True)
        tok_out = jnp.einsum("bdc,ds->bsc", act_full, w2_cols, preferred_element_type=jnp.float32) + b2_part[None, :, None]
        x_mid = (x_wide + tok_out).astype(jnp.bfloat16)
        return channel_mix(x_mid, w_ch1, b_ch1, w_ch2, b_ch2, ln2_gain, ln2_bias)

    in_specs = (row_spec, P("sp", None), P("sp"), P(None, "sp"), P("sp"), P(None, None), P(None), P(None, None), P(None), P(None), P(None), P(None), P(None))
    return jax.shard_map(local_layer, mesh=mesh, in_specs=in_specs, out_specs=row_spec, check_vma=False)
```

profile of v0, /device:TPU:113, one launch (start us, length us, event | category | flops | bytes accessed | tf_op | source)
XLA Modules:
  0.0 721.4 jit_solution(7918696589737632930)
XLA Ops:
  6.5 0.0 copy-start
  6.6 0.1 reduce-scatter.2.cloned.1.call-start
  6.6 32.7 %copy.19 = bf16[32,512,768]{1,2,0:T(8,128)(2,1)} copy(bf16[32,512,768]{2,1,0:T(8,128)(2,1)} %param.13) | data formatting | bytes 50331648 | tf_op args[0]
  39.3 9.7 %convert_reduce_fusion.1 = f32[32,512]{1,0:T(8,128)S(1)} fusion(bf16[32,512,768]{1,2,0:T(8,128)(2,1)} %copy.19), kind=kLoop, calls=%fused_computation.15 | loop fusion | flops 25149440 | bytes 25231360 | tf_op jit(solution)/shard_map/reduce_sum | solution.py:10
  49.0 10.7 %fusion.18 = f32[32,512]{1,0:T(8,128)S(1)} fusion(bf16[32,512,768]{1,2,0:T(8,128)(2,1)} %copy.19, f32[32,512]{1,0:T(8,128)S(1)} %broadcast_multiply_fusion.1), kind=kLoop, calls=%fused_computation.24 | loop fusion | flops 50315264 | bytes 25296896 | tf_op jit(solution)/shard_map/reduce_sum | solution.py:12
  59.8 26.5 %fusion.46 = f32[32,384,768]{1,2,0:T(8,128)} fusion(bf16[32,512,768]{1,2,0:T(8,128)(2,1)} %copy.19, f32[768]{0:T(1024)S(1)} %copy-done.6, f32[768]{0:T(1024)S(1)} %copy-done.7, f32[32,512]{1,0:T(8,128)S(1)} %add_rsqrt_fusion.1, f32[32,512]{1,0:T(8,128)S(1)} %broadcast_multiply_fusion.1, bf16[512,384]{1,0:T(8,128)(2,1)S(1)} %copy-done.4), kind=kOutput, calls=%fused_computation.42 | convolution fusion | flops 9739173888 | bytes 63444992 | tf_op jit(solution)/shard_map/bsc,sd->bdc/dot_general | solution.py:31
  86.4 37.9 %copy.20 = f32[32,384,768]{2,0,1:T(8,128)} copy(f32[32,384,768]{1,2,0:T(8,128)} %fusion.46) | data formatting | bytes 75497472 | tf_op jit(solution)/shard_map/bsc,sd->bdc/transpose | solution.py:31
  124.2 0.1 reduce-scatter.2.cloned.1.call-update
  124.3 0.2 all-gather.2.cloned.1.call-start
  124.5 188.5 %reduce-scatter.2.cloned.1.call-done = f32[32,48,768]{2,0,1:T(8,128)} async-done(((f32[32,384,768]{2,0,1:T(8,128)}), f32[32,48,768]{2,0,1:T(8,128)}) %reduce-scatter.2.cloned.1.call-update) | async-done | bytes 4718608 | tf_op jit(solution)/shard_map/reduce_scatter | solution.py:32
  313.0 5.4 fusion.62
  318.5 0.1 all-gather.2.cloned.1.call-update
  318.5 0.0 copy-start.5
  318.5 0.0 copy-start.8
  318.5 0.0 copy-start.9
  318.6 90.6 %all-gather.2.cloned.1.call-done = bf16[32,384,768]{2,0,1:T(8,128)(2,1)} async-done(((bf16[32,48,768]{2,0,1:T(8,128)(2,1)}), bf16[32,384,768]{2,0,1:T(8,128)(2,1)}) %all-gather.2.cloned.1.call-update) | async-done | bytes 18874384 | tf_op jit(solution)/shard_map/all_gather | solution.py:34
  409.2 29.8 %convert_reduce_fusion = (f32[32,512]{1,0:T(8,128)S(1)}, bf16[32,512,768]{1,2,0:T(8,128)(2,1)}) fusion(f32[512]{0:T(512)S(1)} %copy-done.11, bf16[384,512]{1,0:T(8,128)(2,1)S(1)} %copy-done, bf16[32,384,768]{2,0,1:T(8,128)(2,1)} %all-gather.2.cloned.1.call-done, bf16[32,512,768]{1,2,0:T(8,128)(2,1)} %copy.19), kind=kOutput, calls=%fused_computation.12 | convolution fusion | flops 9739157504 | bytes 69666816 | tf_op jit(solution)/shard_map/bdc,ds->bsc/dot_general | solution.py:35
  439.0 10.7 %fusion.14 = f32[32,512]{1,0:T(8,128)S(1)} fusion(bf16[32,512,768]{1,2,0:T(8,128)(2,1)} %get-tuple-element.6, f32[32,512]{1,0:T(8,128)S(1)} %broadcast_multiply_fusion), kind=kLoop, calls=%fused_computation.20 | loop fusion | flops 50315264 | bytes 25296896 | tf_op jit(solution)/shard_map/reduce_sum | solution.py:12
  449.7 0.0 copy-start.3
  449.7 0.0 copy-start.10
  449.8 142.8 %fusion.81 = bf16[32,512,3072]{2,1,0:T(8,128)(2,1)} fusion(f32[3072]{0:T(1024)S(1)} %copy-done.5, bf16[32,512,768]{1,2,0:T(8,128)(2,1)} %get-tuple-element.6, f32[768]{0:T(1024)S(1)} %copy-done.8, f32[768]{0:T(1024)S(1)} %copy-done.9, f32[32,512]{1,0:T(8,128)S(1)} %add_rsqrt_fusion, f32[32,512]{1,0:T(8,128)S(1)} %broadcast_multiply_fusion, ...), kind=kOutput, calls=%fused_computation.8.clone.clone.clone.clone.1 | convolution fusion | flops 77888225280 | bytes 130697216 | tf_op jit(solution)/shard_map/bsc,cf->bsf/dot_general | solution.py:19
  592.6 0.0 copy-done.10
  592.6 89.4 %fusion.23 = bf16[32,512,768]{1,2,0:T(8,128)(2,1)} fusion(bf16[32,512,768]{1,2,0:T(8,128)(2,1)} %get-tuple-element.6, f32[768]{0:T(1024)S(1)} %copy-done.10, bf16[3072,768]{1,0:T(8,128)(2,1)S(1)} %copy-done.3, bf16[32,512,3072]{2,1,0:T(8,128)(2,1)} %fusion.81), kind=kOutput, calls=%fused_computation.29 | convolution fusion | flops 77359742976 | bytes 155716608 | tf_op jit(solution)/shard_map/bsf,fc->bsc/dot_general | solution.py:21
  682.0 32.6 %copy.24 = bf16[32,512,768]{2,1,0:T(8,128)(2,1)} copy(bf16[32,512,768]{1,2,0:T(8,128)(2,1)} %fusion.23) | data formatting | bytes 50331648 | tf_op jit(solution)/shard_map/convert_element_type | solution.py:22
  (21 shorter events, 0.1 us)
Async XLA Ops:
  6.5 402.6 %copy-start = (bf16[384,512]{1,0:T(8,128)(2,1)S(1)}, bf16[384,512]{1,0:T(8,128)(2,1)}, u32[]{:S(2)}) copy-start(bf16[384,512]{1,0:T(8,128)(2,1)} %param.16) | copy-start | bytes 1179652
  6.6 53.2 %copy-start.6 = (f32[768]{0:T(1024)S(1)}, f32[768]{0:T(1024)}, u32[]{:S(2)}) copy-start(f32[768]{0:T(1024)} %param.23) | copy-start | bytes 9220
  6.6 53.2 %copy-start.7 = (f32[768]{0:T(1024)S(1)}, f32[768]{0:T(1024)}, u32[]{:S(2)}) copy-start(f32[768]{0:T(1024)} %param.22) | copy-start | bytes 9220
  6.6 53.2 %copy-start.4 = (bf16[512,384]{1,0:T(8,128)(2,1)S(1)}, bf16[512,384]{1,0:T(8,128)(2,1)}, u32[]{:S(2)}) copy-start(bf16[512,384]{1,0:T(8,128)(2,1)} %param.14) | copy-start | bytes 1179652
  6.6 306.5 %reduce-scatter.2.cloned.1.call-start = ((), (), s32[]{:S(2)}) async-start(), calls=%async_computation.1 | async-start | bytes 42467328 | tf_op jit(solution)/shard_map/reduce_scatter | solution.py:32
  86.3 226.7 %copy-start.2 = (f32[48]{0:T(128)S(1)}, f32[48]{0:T(128)}, u32[]{:S(2)}) copy-start(f32[48]{0:T(128)} %param.15) | copy-start | bytes 580
  86.4 322.8 %copy-start.11 = (f32[512]{0:T(512)S(1)}, f32[512]{0:T(512)}, u32[]{:S(2)}) copy-start(f32[512]{0:T(512)} %param.17) | copy-start | bytes 6148
  124.3 284.9 %all-gather.2.cloned.1.call-start = ((), (), s32[]{:S(2)}) async-start(), calls=%async_computation.2 | async-start | bytes 21233664 | tf_op jit(solution)/shard_map/all_gather | solution.py:34
  318.5 131.2 %copy-start.5 = (f32[3072]{0:T(1024)S(1)}, f32[3072]{0:T(1024)}, u32[]{:S(2)}) copy-start(f32[3072]{0:T(1024)} %param.19) | copy-start | bytes 36868
  318.5 131.2 %copy-start.8 = (f32[768]{0:T(1024)S(1)}, f32[768]{0:T(1024)}, u32[]{:S(2)}) copy-start(f32[768]{0:T(1024)} %param.25) | copy-start | bytes 9220
  318.5 131.2 %copy-start.9 = (f32[768]{0:T(1024)S(1)}, f32[768]{0:T(1024)}, u32[]{:S(2)}) copy-start(f32[768]{0:T(1024)} %param.24) | copy-start | bytes 9220
  449.7 142.8 %copy-start.3 = (bf16[3072,768]{1,0:T(8,128)(2,1)S(1)}, bf16[3072,768]{1,0:T(8,128)(2,1)}, u32[]{:S(2)}) copy-start(bf16[3072,768]{1,0:T(8,128)(2,1)} %param.20) | copy-start | bytes 14155780
  449.7 142.8 %copy-start.10 = (f32[768]{0:T(1024)S(1)}, f32[768]{0:T(1024)}, u32[]{:S(2)}) copy-start(f32[768]{0:T(1024)} %param.21) | copy-start | bytes 9220
  592.6 122.0 %copy-start.1 = (bf16[384,512]{1,0:T(8,128)(2,1)S(1)}, bf16[384,512]{1,0:T(8,128)(2,1)}, u32[]{:S(2)}) copy-start(bf16[384,512]{1,0:T(8,128)(2,1)} %param.16) | copy-start | bytes 1179652
Sparse Core Ops, SparseCore 0:
  124.4 188.5 reduce-scatter.1
  318.6 90.4 all-gather.1
where the time goes:
time: 724 us; the launch traced here: 721 us
  matrix products  289 us (40%)
  waiting for transfers between devices  279 us (39%)
  local copies, waits for them, and re-layouts  103 us (14%)
  other arithmetic  36.6 us (5%)
  between operations  13.6 us (2%)
    reduce_scatter x1, waiting for transfers between devices, local_layer(): lax.psum_scatter(part_pre, 'sp', scatter_dimension=1, tiled=True)  188 us
    dot_general x1, matrix products, channel_mix(): jnp.einsum('bsc,cf->bsf', normed_two, w_ch1, preferred_element_type=jnp.f...  143 us
    all_gather x1, waiting for transfers between devices, local_layer(): act_full = lax.all_gather(tok_act, 'sp', axis=1, tiled=True)  90.6 us
    dot_general x1, matrix products, channel_mix(): jnp.einsum('bsf,fc->bsc', ch_act, w_ch2, preferred_element_type=jnp.float32)  89.4 us
    transpose x1, local copies, waits for them, and re-layouts, local_layer(): jnp.einsum('bsc,sd->bdc', normed, w1_rows, preferred_element_type=jnp.flo...  37.9 us
    unnamed x25, local copies, waits for them, and re-layouts  32.8 us
    convert_element_type x1, local copies, waits for them, and re-layouts, channel_mix(): return (mid_wide + ch_out).astype(jnp.bfloat16)  32.6 us
    dot_general x1, matrix products, local_layer(): jnp.einsum('bdc,ds->bsc', act_full, w2_cols, preferred_element_type=jnp.f...  29.8 us
  transfers between devices with their start and end apart: 2, of which 2 were waited for; matrix products, arithmetic and copies ran while one was open for 0% of the time, Pallas kernels for 0%

commit v1 on v0

v1 whole, which is shorter than its diff:
```python
import functools

import jax
import jax.numpy as jnp
from jax import lax
from jax.experimental import pallas as pl
from jax.experimental.pallas import tpu as pltpu
from jax.sharding import PartitionSpec as P

LN_EPS = 1e-6
GELU_A = 0.7978845608028654
GELU_B = 0.7978845608028654 * 0.044715


def gelu(v):
    inner = v * (GELU_A + GELU_B * (v * v))
    return (0.5 * v) * (1.0 + jnp.tanh(inner))


def layer_norm(values, gain, bias):
    width = values.shape[-1]
    mean = jnp.sum(values, axis=-1, keepdims=True) * (1.0 / width)
    centred = values - mean
    var = jnp.sum(centred * centred, axis=-1, keepdims=True) * (1.0 / width)
    return centred * lax.rsqrt(var + LN_EPS) * gain + bias


def dot(a, b):
    return lax.dot_general(a, b, (((1,), (0,)), ((), ())), preferred_element_type=jnp.float32)


def first_kernel(x_ref, w_ref, gain_ref, bias_ref, o_ref, u_ref):
    rows = x_ref.shape[1]
    for r in range(0, rows, 64):
        xs = x_ref[0, r:r + 64, :].astype(jnp.float32)
        u_ref[r:r + 64, :] = layer_norm(xs, gain_ref[...], bias_ref[...]).astype(jnp.bfloat16)
    o_ref[0] = dot(w_ref[...], u_ref[...])


def first_call(x, w1t, gain, bias):
    n, s, c = x.shape
    d = w1t.shape[0]
    return pl.pallas_call(
        first_kernel,
        grid=(n,),
        out_shape=jax.ShapeDtypeStruct((n, d, c), jnp.float32),
        in_specs=[
            pl.BlockSpec((1, s, c), lambda i: (i, 0, 0)),
            pl.BlockSpec((d, s), lambda i: (0, 0)),
            pl.BlockSpec((1, c), lambda i: (0, 0)),
            pl.BlockSpec((1, c), lambda i: (0, 0)),
        ],
        out_specs=pl.BlockSpec((1, d, c), lambda i: (i, 0, 0)),
        scratch_shapes=[pltpu.VMEM((s, c), jnp.bfloat16)],
    )(x, w1t, gain, bias)


def second_kernel(n_img, x_hbm, g_hbm, w2t_hbm, wc1_hbm, wc2_hbm, b2_ref, bc1_ref, bc2_ref, gain_ref, bias_ref, z_hbm,
                  xb, gb, zb, w2t, wc1, wc2, tbuf, x1, vn, v, a0, a1, a2, acc, sem_x, sem_g, sem_z, sem_w):
    def load_x(i):
        return pltpu.make_async_copy(x_hbm.at[i], xb.at[lax.rem(i, 2)], sem_x.at[lax.rem(i, 2)])

    def load_g(i):
        return pltpu.make_async_copy(g_hbm.at[i], gb.at[lax.rem(i, 2)], sem_g.at[lax.rem(i, 2)])

    def store_z(i):
        return pltpu.make_async_copy(zb.at[lax.rem(i, 2)], z_hbm.at[i], sem_z.at[lax.rem(i, 2)])

    weights = [pltpu.make_async_copy(s, d, sem_w.at[k]) for k, (s, d) in enumerate(
        [(w2t_hbm, w2t), (wc1_hbm, wc1), (wc2_hbm, wc2)])]
    load_x(0).start()
    load_g(0).start()
    for w in weights:
        w.start()
    load_x(1).start()
    load_g(1).start()

    rows = x1.shape[0]
    abufs = (a0, a1, a2)
    wide = a0.shape[1]

    def token_mix(slot):
        gv = gb[slot]
        for c in range(0, 768, 256):
            tbuf[:, c:c + 256] = dot(w2t[...], gv[:, c:c + 256])
        for r in range(0, rows, 64):
            xs = xb[slot, r:r + 64, :].astype(jnp.float32)
            x_mid = (xs + (tbuf[r:r + 64, :] + b2_ref[r:r + 64, :])).astype(jnp.bfloat16)
            x1[r:r + 64, :] = x_mid
            vn[r:r + 64, :] = layer_norm(x_mid.astype(jnp.float32), gain_ref[...], bias_ref[...]).astype(jnp.bfloat16)

    def p1(s, src):
        for c in range(0, wide, 256):
            k = s * wide + c
            pre = dot(src[...], wc1[:, k:k + 256]) + bc1_ref[:, k:k + 256]
            abufs[s][:, c:c + 256] = gelu(pre).astype(jnp.bfloat16)

    def p2(s, slot=None):
        for c in range(0, 768, 256):
            part = dot(abufs[s][...], wc2[s * wide:(s + 1) * wide, c:c + 256])
            if s == 0:
                acc[:, c:c + 256] = part + (x1[:, c:c + 256].astype(jnp.float32) + bc2_ref[:, c:c + 256])
            elif s == 1:
                acc[:, c:c + 256] += part
            else:
                zb[slot, :, c:c + 256] = (acc[:, c:c + 256] + part).astype(jnp.bfloat16)

    load_x(0).wait()
    load_g(0).wait()
    weights[0].wait()
    token_mix(0)
    weights[1].wait()
    weights[2].wait()

    def body(n, _):
        prev = n - 1
        slot = lax.rem(n + 1, 2)

        @pl.when(n >= 3)
        def _():
            store_z(n - 3).wait()

        p1(0, vn)
        v[...] = vn[...]
        p2(2, slot)
        @pl.when(n >= 1)
        def _():
            store_z(prev).start()

        @pl.when(n + 1 < n_img)
        def _():
            load_x(n + 1).wait()
            load_g(n + 1).wait()

        p1(1, v)
        p2(0)
        p1(2, v)
        p2(1)
        token_mix(slot)

        @pl.when(n + 2 < n_img)
        def _():
            load_x(n + 2).start()
            load_g(n + 2).start()

        return 0

    lax.fori_loop(0, n_img, body, 0)
    last = n_img - 1
    store_z(last - 2).wait()
    p2(2, last % 2)
    store_z(last).start()
    store_z(last - 1).wait()
    store_z(last).wait()


def second_call(x, g, w2t, wc1, wc2, b2, bc1, bc2, gain, bias):
    n, s, c = x.shape
    d = g.shape[1]
    f = wc1.shape[1]
    any_spec = pl.BlockSpec(memory_space=pl.ANY)
    vm = pl.BlockSpec(memory_space=pltpu.VMEM)
    bf, f32 = jnp.bfloat16, jnp.float32
    return pl.pallas_call(
        functools.partial(second_kernel, n),
        out_shape=jax.ShapeDtypeStruct((n, s, c), bf),
        in_specs=[any_spec] * 5 + [vm] * 5,
        out_specs=any_spec,
        scratch_shapes=[
            pltpu.VMEM((2, s, c), bf), pltpu.VMEM((2, d, c), bf), pltpu.VMEM((2, s, c), bf),
            pltpu.VMEM((s, d), bf), pltpu.VMEM((c, f), bf), pltpu.VMEM((f, c), bf),
            pltpu.VMEM((s, c), f32), pltpu.VMEM((s, c), bf), pltpu.VMEM((s, c), bf), pltpu.VMEM((s, c), bf),
            pltpu.VMEM((s, f // 3), bf), pltpu.VMEM((s, f // 3), bf), pltpu.VMEM((s, f // 3), bf),
            pltpu.VMEM((s, c), f32),
            pltpu.SemaphoreType.DMA((2,)), pltpu.SemaphoreType.DMA((2,)), pltpu.SemaphoreType.DMA((2,)),
            pltpu.SemaphoreType.DMA((3,)),
        ],
        compiler_params=pltpu.CompilerParams(vmem_limit_bytes=60 * 1024 * 1024),
    )(x, g, w2t, wc1, wc2, b2, bc1, bc2, gain, bias)


def solution(mesh):
    row_spec = P("dp", "sp", None)

    def local_layer(x_blk, w1_rows, b1_part, w2_cols, b2_part, w_ch1, b_ch1, w_ch2, b_ch2, ln1_gain, ln1_bias, ln2_gain, ln2_bias):
        part_pre = first_call(x_blk, w1_rows.T, ln1_gain[None], ln1_bias[None])
        tok_pre = lax.psum_scatter(part_pre, "sp", scatter_dimension=1, tiled=True) + b1_part[None, :, None]
        tok_act = gelu(tok_pre).astype(jnp.bfloat16)
        act_full = lax.all_gather(tok_act, "sp", axis=1, tiled=True)
        return second_call(x_blk, act_full, w2_cols.T, w_ch1, w_ch2, b2_part[:, None], b_ch1[None], b_ch2[None],
                           ln2_gain[None], ln2_bias[None])

    in_specs = (row_spec, P("sp", None), P("sp"), P(None, "sp"), P("sp"), P(None, None), P(None), P(None, None), P(None), P(None), P(None), P(None), P(None))
    return jax.shard_map(local_layer, mesh=mesh, in_specs=in_specs, out_specs=row_spec, check_vma=False)
```

time: 724 us -> 570 us (0.79)
  matrix products: 289 us -> 0 us
  Pallas kernels: 0 us -> 266 us
  local copies, waits for them, and re-layouts: 103 us -> 8.08 us
  other arithmetic: 36.6 us -> 5.25 us
    dot_general x4 -> x0, matrix products: 289 us -> none  [the longest x1 143 us: channel_mix(): jnp.einsum('bsc,cf->bsf', normed_two, w_ch1, preferred_element_type=jnp.f...]
    pallas_call x0 -> x2, Pallas kernels: none -> 266 us  [the longest x1 224 us: second_call(): pl.pallas_call(functools.partial(second_kernel, n), out_shape=jax.ShapeDt...]
    transpose x1 -> x0, local copies, waits for them, and re-layouts: 37.9 us -> none  [local_layer(): jnp.einsum('bsc,sd->bdc', normed, w1_rows, preferred_element_type=jnp.flo...]
    convert_element_type x1 -> x0, local copies, waits for them, and re-layouts: 32.6 us -> none  [channel_mix(): return (mid_wide + ch_out).astype(jnp.bfloat16)]
    reduce_sum x3 -> x0, other arithmetic: 31.1 us -> none  [the longest x2 21.4 us: layer_norm(): var_val = jnp.mean(centred * centred, axis=-1, keepdims=True)]
    unnamed x25 -> x14, local copies, waits for them, and re-layouts: 32.8 us -> 2.87 us
  transfers between devices with their start and end apart: 2 -> 2, of which waited for: 2 -> 2; matrix products, arithmetic and copies ran while one was open for 0% -> 1% of each run, Pallas kernels for 0% -> 0%
where the time goes in v1:
time: 570 us; the launch traced here: 568 us
  waiting for transfers between devices  276 us (48%)
  Pallas kernels  266 us (47%)
  between operations  13.5 us (2%)
  local copies, waits for them, and re-layouts  8.08 us (1%)
    pallas_call x1, Pallas kernels, second_call(): pl.pallas_call(functools.partial(second_kernel, n), out_shape=jax.ShapeDt...  224 us
    reduce_scatter x1, waiting for transfers between devices, local_layer(): lax.psum_scatter(part_pre, 'sp', scatter_dimension=1, tiled=True)  189 us
    all_gather x1, waiting for transfers between devices, local_layer(): act_full = lax.all_gather(tok_act, 'sp', axis=1, tiled=True)  87.1 us
    pallas_call x1, Pallas kernels, first_call(): pl.pallas_call(first_kernel, grid=(n,), out_shape=jax.ShapeDtypeStruct((n...  41.9 us
  transfers between devices with their start and end apart: 2, of which 2 were waited for; matrix products, arithmetic and copies ran while one was open for 1% of the time, Pallas kernels for 0%

profile of v1, /device:TPU:113, one launch (start us, length us, event | category | flops | bytes accessed | tf_op | source)
XLA Modules:
  0.0 568.4 jit_solution(6353665624415173498)
XLA Ops:
  6.5 0.0 reduce-scatter.2.cloned.1.call-start
  6.6 1.3 broadcast_in_dim.22.gain_ref
  7.8 1.3 broadcast_in_dim.23.bias_ref
  9.1 1.9 copy.16
  11.0 41.9 %shard_map.127 = f32[32,384,768]{2,1,0:T(8,128)} custom-call(bf16[32,512,768]{2,1,0:T(8,128)(2,1)} %x_hbm.1, bf16[384,512]{1,0:T(8,128)(2,1)} %bitcast.5, f32[1,768]{1,0:T(1,128)} %broadcast_in_dim.22.gain_ref, f32[1,768]{1,0:T(1,128)} %broadcast_in_dim.23.bias_ref), custom_call_target="tpu_custom_call" | custom-call | tf_op jit(solution)/shard_map/pallas_call | solution.py:43
  53.0 0.1 reduce-scatter.2.cloned.1.call-update
  53.0 0.0 copy-start.1
  53.0 0.0 copy-start.2
  53.0 0.0 copy-start.3
  53.1 0.0 copy-start.4
  53.1 0.0 copy-start
  53.1 0.1 all-gather.2.cloned.1.call-start
  53.2 188.6 %reduce-scatter.2.cloned.1.call-done = f32[32,48,768]{2,1,0:T(8,128)} async-done(((f32[32,384,768]{2,1,0:T(8,128)}), f32[32,48,768]{2,1,0:T(8,128)}) %reduce-scatter.2.cloned.1.call-update) | async-done | bytes 4718608 | tf_op jit(solution)/shard_map/reduce_scatter | solution.py:187
  241.8 0.0 copy-done.5
  241.8 5.3 multiply_convert_fusion
  247.0 0.1 all-gather.2.cloned.1.call-update
  247.1 0.6 broadcast_in_dim.26.bc2_ref
  247.7 0.6 broadcast_in_dim.27.gain_ref
  248.3 0.6 broadcast_in_dim.28.bias_ref
  248.9 0.9 copy.18.b2_ref
  249.7 0.0 copy-done
  249.7 0.9 copy.17
  250.7 87.1 %all-gather.2.cloned.1.call-done.g_hbm = bf16[32,384,768]{2,1,0:T(8,128)(2,1)} async-done(((bf16[32,48,768]{2,1,0:T(8,128)(2,1)}), bf16[32,384,768]{2,1,0:T(8,128)(2,1)}) %all-gather.2.cloned.1.call-update) | async-done | bytes 18874384 | tf_op jit(solution)/shard_map/all_gather | solution.py:189
  337.7 223.8 %shard_map.128 = bf16[32,512,768]{2,1,0:T(8,128)(2,1)} custom-call(bf16[32,512,768]{2,1,0:T(8,128)(2,1)} %x_hbm.1, bf16[32,384,768]{2,1,0:T(8,128)(2,1)} %all-gather.2.cloned.1.call-done.g_hbm, bf16[512,384]{1,0:T(8,128)(2,1)} %bitcast.4, bf16[768,3072]{1,0:T(8,128)(2,1)} %wc1_hbm.1, bf16[3072,768]{1,0:T(8,128)(2,1)} %wc2_hbm.1, f32[512,1]{1,0:T(8,128)} %copy.18.b2_ref, ...), custom_call_target="tpu_custom_call" | custom-call | tf_op jit(solution)/shard_map/pallas_call | solution.py:164
  (5 shorter events, 0.0 us)
Async XLA Ops:
  6.5 235.2 %reduce-scatter.2.cloned.1.call-start = ((), (), s32[]{:S(2)}) async-start(), calls=%async_computation.1 | async-start | bytes 42467328 | tf_op jit(solution)/shard_map/reduce_scatter | solution.py:187
  53.0 188.8 %copy-start.5 = (f32[48]{0:T(128)S(1)}, f32[48]{0:T(128)}, u32[]{:S(2)}) copy-start(f32[48]{0:T(128)} %param.15) | copy-start | bytes 580
  53.0 194.1 %copy-start.1 = (f32[768]{0:T(1024)S(1)}, f32[768]{0:T(1024)}, u32[]{:S(2)}) copy-start(f32[768]{0:T(1024)} %param.21) | copy-start | bytes 9220
  53.0 194.6 %copy-start.2 = (f32[768]{0:T(1024)S(1)}, f32[768]{0:T(1024)}, u32[]{:S(2)}) copy-start(f32[768]{0:T(1024)} %param.24) | copy-start | bytes 9220
  53.0 195.2 %copy-start.3 = (f32[768]{0:T(1024)S(1)}, f32[768]{0:T(1024)}, u32[]{:S(2)}) copy-start(f32[768]{0:T(1024)} %param.25) | copy-start | bytes 9220
  53.1 195.8 %copy-start.4 = (f32[512]{0:T(512)S(1)}, f32[512]{0:T(512)}, u32[]{:S(2)}) copy-start(f32[512]{0:T(512)} %param.17) | copy-start | bytes 6148
  53.1 196.7 %copy-start = (bf16[384,512]{1,0:T(8,128)(2,1)S(1)}, bf16[384,512]{1,0:T(8,128)(2,1)}, u32[]{:S(2)}) copy-start(bf16[384,512]{1,0:T(8,128)(2,1)} %param.16) | copy-start | bytes 1179652
  53.1 284.7 %all-gather.2.cloned.1.call-start = ((), (), s32[]{:S(2)}) async-start(), calls=%async_computation.2 | async-start | bytes 21233664 | tf_op jit(solution)/shard_map/all_gather | solution.py:189
Sparse Core Ops, SparseCore 0:
  53.1 188.5 reduce-scatter.1
  247.2 90.4 all-gather.1

commit v2 on v0

v2 whole, which is shorter than its diff:
```python
import functools

import jax
import jax.numpy as jnp
from jax import lax
from jax.experimental import pallas as pl
from jax.experimental.pallas import tpu as pltpu
from jax.sharding import PartitionSpec as P

LN_EPS = 1e-6
GELU_A = 0.7978845608028654
GELU_B = 0.7978845608028654 * 0.044715
BF, F32 = jnp.bfloat16, jnp.float32
SLOTS = 8
SEND_PAIR, SUM_PAIR, SEND_FAR, SUM_FAR, SEND_NEAR, SUM_NEAR = 1, 2, 3, 4, 5, 7
SEND_ACT, FORWARD, FORWARD_FAR, TOKEN, MAIN = 8, 10, 11, 12, 13


def gelu(v):
    inner = v * (GELU_A + GELU_B * (v * v))
    return (0.5 * v) * (1.0 + jnp.tanh(inner))


def layer_norm(values, gain, bias):
    width = values.shape[-1]
    mean = jnp.sum(values, axis=-1, keepdims=True) * (1.0 / width)
    centred = values - mean
    var = jnp.sum(centred * centred, axis=-1, keepdims=True) * (1.0 / width)
    return centred * lax.rsqrt(var + LN_EPS) * gain + bias


def dot(a, b):
    return lax.dot_general(a, b, (((1,), (0,)), ((), ())), preferred_element_type=F32)


def kernel(n_img, x_hbm, w1t_hbm, w2t_hbm, wc1_hbm, wc2_hbm, b1_ref, b2_ref, bc1_ref, bc2_ref,
           gain1_ref, bias1_ref, gain2_ref, bias2_ref, z_hbm,
           xa, xt, zb, w1p, w2t, wc1, wc2, u, own, pair_out, pair_in, q0, q1, far_out, far_in, near_out, near_in, act,
           tbuf, x1, vn, v, a0, a1, a2, acc, sem_xa, sem_xt, sem_z, sem_w, send_sems, recv_sems):
    rows, chan = x1.shape
    half = chan // 2
    part = act.shape[2]
    n_dev = act.shape[1]
    me = lax.axis_index("sp")
    core = lax.rem(me, 2)
    sib = me + 1 - 2 * core
    up = lax.rem(me + 2, n_dev)
    down = lax.rem(me + n_dev - 2, n_dev)
    far = lax.rem(me + 4, n_dev)

    def s8(i):
        return lax.rem(i, SLOTS)

    def s4(i):
        return lax.rem(i, 4)

    def remote(kind, i, src, dst, to):
        return pltpu.make_async_remote_copy(
            src_ref=src, dst_ref=dst, send_sem=send_sems.at[kind, s8(i)], recv_sem=recv_sems.at[kind, s8(i)],
            device_id={"sp": to}, device_id_type=pl.DeviceIdType.MESH)

    lo, hi = pl.ds(0, half), pl.ds(half, half)

    def out_pair(i):
        return [remote(0, i, pair_out.at[s4(i)], pair_in.at[s8(i)], sib)]

    def out_far(i):
        return [remote(1, i, far_out.at[s4(i), 0], far_in.at[s8(i), 0], up),
                remote(2, i, far_out.at[s4(i), 1], far_in.at[s8(i), 1], down)]

    def out_near(i):
        return [remote(3, i, near_out.at[s4(i), 0], near_in.at[s8(i), 0], up),
                remote(4, i, near_out.at[s4(i), 1], near_in.at[s8(i), 1], down)]

    def block(i, k):
        return act.at[s8(i), k]

    def out_act(i):
        b = block(i, me)
        return [remote(5, i, b, b, up), remote(6, i, b, b, down), remote(7, i, b, b, sib)]

    def out_forward(i):
        lower, upper = block(i, down), block(i, up)
        lower_half, upper_half = act.at[s8(i), down, :, lo], act.at[s8(i), up, :, hi]
        return [remote(8, i, lower_half, lower_half, up), remote(9, i, upper_half, upper_half, down),
                remote(10, i, lower, lower, sib), remote(11, i, upper, upper, sib)]

    def out_forward_far(i):
        b = block(i, far)
        return [remote(12, i, b, b, sib)]

    def in_act(i):
        lower, upper = block(i, down), block(i, up)
        return [remote(5, i, lower, lower, up), remote(6, i, upper, upper, down)]

    def in_forward(i):
        a, b = act.at[s8(i), far, :, lo], act.at[s8(i), far, :, hi]
        return [remote(8, i, a, a, up), remote(9, i, b, b, down)]

    def in_sib(i):
        def pairof(k):
            return k + 1 - 2 * core
        return [remote(kind, i, block(i, pairof(k)), block(i, pairof(k)), sib)
                for kind, k in ((7, me), (10, down), (11, up), (12, far))]

    def load_xa(i):
        return pltpu.make_async_copy(x_hbm.at[i], xa.at[s4(i)], sem_xa.at[s4(i)])

    def load_xt(i):
        return pltpu.make_async_copy(x_hbm.at[i], xt.at[lax.rem(i, 2)], sem_xt.at[lax.rem(i, 2)])

    def store_z(i):
        return pltpu.make_async_copy(zb.at[lax.rem(i, 3)], z_hbm.at[i], sem_z.at[lax.rem(i, 3)])

    w_copies = []
    for r in range(n_dev):
        to = lax.rem(me - core + 2 * r, n_dev) if r < 4 else lax.rem(me - core + 2 * (r - 4), n_dev)
        k = to + core if r < 4 else to + 1 - core
        w_copies.append(pltpu.make_async_copy(
            w1t_hbm.at[k], w1p.at[pl.ds(r * part, part), :], sem_w.at[r]))
    load_xa(0).start()
    for c in w_copies:
        c.start()
    load_xa(1).start()
    big = [pltpu.make_async_copy(s, d, sem_w.at[n_dev + k]) for k, (s, d) in enumerate(
        [(w2t_hbm, w2t), (wc1_hbm, wc1), (wc2_hbm, wc2)])]
    for c in big:
        c.start()

    barrier = pltpu.get_barrier_semaphore()
    for peer in (sib, up, down):
        pl.semaphore_signal(barrier, inc=1, device_id={"sp": peer}, device_id_type=pl.DeviceIdType.MESH)
    pl.semaphore_wait(barrier, 3)
    for c in w_copies:
        c.wait()

    def norm_one(i):
        slot = s4(i)
        for r in range(0, rows, 64):
            xs = xa[slot, r:r + 64, :].astype(F32)
            u[r:r + 64, :] = layer_norm(xs, gain1_ref[...], bias1_ref[...]).astype(BF)

    def partial(i):
        slot = s4(i)
        for c in range(0, chan, 256):
            p = dot(w1p[...], u[:, c:c + 256])
            for r in range(4):
                own[slot, r, :, c:c + 256] = p[r * part:(r + 1) * part]
                pair_out[slot, r, :, c:c + 256] = p[(4 + r) * part:(5 + r) * part].astype(BF)

    def sum_pair(i):
        slot, big_slot = s4(i), s8(i)
        def total(r):
            return own[slot, r] + pair_in[big_slot, r].astype(F32)
        q0[big_slot] = total(0)
        q1[big_slot, 0] = total(1)
        q1[big_slot, 1] = total(3)
        t = total(2).astype(BF)
        far_out[slot, 0] = t[:, :half]
        far_out[slot, 1] = t[:, half:]

    def sum_far(i):
        slot, big_slot = s4(i), s8(i)
        near_out[slot, 0, :, :half] = (q1[big_slot, 0, :, :half] + far_in[big_slot, 0].astype(F32)).astype(BF)
        near_out[slot, 0, :, half:] = q1[big_slot, 0, :, half:].astype(BF)
        near_out[slot, 1, :, :half] = q1[big_slot, 1, :, :half].astype(BF)
        near_out[slot, 1, :, half:] = (q1[big_slot, 1, :, half:] + far_in[big_slot, 1].astype(F32)).astype(BF)

    def sum_near(i):
        slot = s8(i)
        for c in range(0, chan, 256):
            h = (q0[slot, :, c:c + 256] + near_in[slot, 0, :, c:c + 256].astype(F32)
                 + near_in[slot, 1, :, c:c + 256].astype(F32)) + b1_ref[...]
            act[slot, me, :, c:c + 256] = gelu(h).astype(BF)

    def token_dot(i):
        gv = act[s8(i)].reshape(n_dev * part, chan)
        for c in range(0, chan, 256):
            tbuf[:, c:c + 256] = dot(w2t[...], gv[:, c:c + 256])

    def norm_two(i):
        slot = lax.rem(i, 2)
        for r in range(0, rows, 64):
            xs = xt[slot, r:r + 64, :].astype(F32)
            x_mid = (xs + (tbuf[r:r + 64, :] + b2_ref[r:r + 64, :])).astype(BF)
            x1[r:r + 64, :] = x_mid
            vn[r:r + 64, :] = layer_norm(x_mid.astype(F32), gain2_ref[...], bias2_ref[...]).astype(BF)

    abufs = (a0, a1, a2)
    wide = a0.shape[1]

    def p1(s, src):
        for c in range(0, wide, 256):
            k = s * wide + c
            pre = dot(src[...], wc1[:, k:k + 256]) + bc1_ref[:, k:k + 256]
            abufs[s][:, c:c + 256] = gelu(pre).astype(BF)

    def p2(s, slot=None):
        for c in range(0, chan, 256):
            piece = dot(abufs[s][...], wc2[s * wide:(s + 1) * wide, c:c + 256])
            if s == 0:
                acc[:, c:c + 256] = piece + (x1[:, c:c + 256].astype(F32) + bc2_ref[:, c:c + 256])
            elif s == 1:
                acc[:, c:c + 256] += piece
            else:
                zb[slot, :, c:c + 256] = (acc[:, c:c + 256] + piece).astype(BF)

    def boundary(t, when):
        def each(i, make, method):
            def run(j):
                for c in make(j):
                    getattr(c, method)()
            when(i, run)

        def sends(lag, make):
            each(t - lag - 2, make, "wait_send")
            each(t - lag, make, "start")

        def arrives(lag, make):
            each(t - lag, make, "wait_recv")

        arrives(SUM_FAR, out_far)
        arrives(FORWARD_FAR, in_forward)
        arrives(FORWARD, in_act)
        arrives(SUM_NEAR, out_near)
        sends(SEND_FAR, out_far)
        sends(FORWARD, out_forward)
        sends(SEND_NEAR, out_near)
        sends(SEND_ACT, out_act)
        sends(FORWARD_FAR, out_forward_far)
        sends(SEND_PAIR, out_pair)
        arrives(SUM_PAIR, out_pair)
        arrives(TOKEN, in_sib)
        when(t, lambda i: load_xa(i).wait())
        when(t + 2, lambda i: load_xa(i).start(), edge=True)
        when(t - TOKEN, lambda i: load_xt(i).wait())
        when(t - TOKEN + 1, lambda i: load_xt(i).start())
        when(t - MAIN - 4, lambda i: store_z(i).wait(), edge=True)
        when(t - MAIN - 2, lambda i: store_z(i).start(), edge=True)

    def guard(i, fn, edge=True):
        @pl.when(jnp.logical_and(i >= 0, i < n_img))
        def _():
            fn(i)

    def start_up(t, _):
        boundary(t, guard)
        guard(t - SUM_NEAR, sum_near)
        guard(t - SUM_FAR, sum_far)
        guard(t - SUM_PAIR, sum_pair)
        norm_one(t)
        partial(t)

        @pl.when(t == TOKEN)
        def _():
            big[0].wait()
            token_dot(t - TOKEN)
            norm_two(t - TOKEN)
        return 0

    lax.fori_loop(0, MAIN, start_up, 0)
    big[1].wait()
    big[2].wait()

    def steady(t, _):
        boundary(t, lambda i, fn, edge=False: guard(i, fn) if edge else fn(i))
        n = t - MAIN
        norm_one(t)
        p1(0, vn)
        v[...] = vn[...]
        p2(2, lax.rem(n + 2, 3))
        token_dot(n + 1)
        partial(t)
        sum_pair(t - SUM_PAIR)
        p1(1, v)
        p2(0)
        norm_two(n + 1)
        sum_far(t - SUM_FAR)
        sum_near(t - SUM_NEAR)
        p1(2, v)
        p2(1)
        return 0

    lax.fori_loop(MAIN, n_img, steady, 0)

    def drain(t, _):
        boundary(t, guard)
        n = t - MAIN
        guard(t - SUM_PAIR, sum_pair)
        guard(t - SUM_FAR, sum_far)
        guard(t - SUM_NEAR, sum_near)
        p1(0, vn)
        v[...] = vn[...]
        p2(2, lax.rem(n + 2, 3))
        token_dot(n + 1)
        p1(1, v)
        p2(0)
        norm_two(n + 1)
        p1(2, v)
        p2(1)
        return 0

    lax.fori_loop(n_img, n_img + MAIN, drain, 0)
    store_z(n_img - 2).start()
    store_z(n_img - 4).wait()
    p2(2, (n_img - 1) % 3)
    store_z(n_img - 1).start()
    for i in (n_img - 3, n_img - 2, n_img - 1):
        store_z(i).wait()


def layer_call(x, w1t, w2t, wc1, wc2, b1, b2, bc1, bc2, gain1, bias1, gain2, bias2):
    n, s, c = x.shape
    n_dev, part, _ = w1t.shape
    d = n_dev * part
    f = wc1.shape[1]
    any_spec = pl.BlockSpec(memory_space=pl.ANY)
    vm = pl.BlockSpec(memory_space=pltpu.VMEM)
    half = c // 2
    return pl.pallas_call(
        functools.partial(kernel, n),
        out_shape=jax.ShapeDtypeStruct((n, s, c), BF),
        in_specs=[any_spec] * 5 + [vm] * 8,
        out_specs=any_spec,
        scratch_shapes=[
            pltpu.VMEM((4, s, c), BF), pltpu.VMEM((2, s, c), BF), pltpu.VMEM((3, s, c), BF),
            pltpu.VMEM((d, s), BF), pltpu.VMEM((s, d), BF), pltpu.VMEM((c, f), BF), pltpu.VMEM((f, c), BF),
            pltpu.VMEM((s, c), BF),
            pltpu.VMEM((4, 4, part, c), F32), pltpu.VMEM((4, 4, part, c), BF), pltpu.VMEM((SLOTS, 4, part, c), BF),
            pltpu.VMEM((SLOTS, part, c), F32), pltpu.VMEM((SLOTS, 2, part, c), F32),
            pltpu.VMEM((4, 2, part, half), BF), pltpu.VMEM((SLOTS, 2, part, half), BF),
            pltpu.VMEM((4, 2, part, c), BF), pltpu.VMEM((SLOTS, 2, part, c), BF),
            pltpu.VMEM((SLOTS, n_dev, part, c), BF),
            pltpu.VMEM((s, c), F32), pltpu.VMEM((s, c), BF), pltpu.VMEM((s, c), BF), pltpu.VMEM((s, c), BF),
            pltpu.VMEM((s, f // 3), BF), pltpu.VMEM((s, f // 3), BF), pltpu.VMEM((s, f // 3), BF),
            pltpu.VMEM((s, c), F32),
            pltpu.SemaphoreType.DMA((4,)), pltpu.SemaphoreType.DMA((2,)), pltpu.SemaphoreType.DMA((3,)),
            pltpu.SemaphoreType.DMA((n_dev + 3,)),
            pltpu.SemaphoreType.DMA((13, SLOTS)), pltpu.SemaphoreType.DMA((13, SLOTS)),
        ],
        compiler_params=pltpu.CompilerParams(vmem_limit_bytes=62 * 1024 * 1024, collective_id=0, has_side_effects=True),
    )(x, w1t, w2t, wc1, wc2, b1, b2, bc1, bc2, gain1, bias1, gain2, bias2)


def solution(mesh):
    row_spec = P("dp", "sp", None)
    n_dev = mesh.shape["sp"]

    def local_layer(x_blk, w1_rows, b1_part, w2_cols, b2_part, w_ch1, b_ch1, w_ch2, b_ch2, ln1_gain, ln1_bias, ln2_gain, ln2_bias):
        s, d = w1_rows.shape
        return layer_call(x_blk, w1_rows.T.reshape(n_dev, d // n_dev, s), w2_cols.T, w_ch1, w_ch2,
                          b1_part[:, None], b2_part[:, None], b_ch1[None], b_ch2[None],
                          ln1_gain[None], ln1_bias[None], ln2_gain[None], ln2_bias[None])

    in_specs = (row_spec, P("sp", None), P("sp"), P(None, "sp"), P("sp"), P(None, None), P(None), P(None, None), P(None), P(None), P(None), P(None), P(None))
    return jax.shard_map(local_layer, mesh=mesh, in_specs=in_specs, out_specs=row_spec, check_vma=False)
```

time: 724 us -> 311 us (0.43)
  matrix products: 289 us -> 0 us
  waiting for transfers between devices: 279 us -> 0 us
  Pallas kernels: 0 us -> 275 us
  local copies, waits for them, and re-layouts: 103 us -> 33.6 us
  other arithmetic: 36.6 us -> 0 us
  between operations: 13.6 us -> 0.01 us
    dot_general x4 -> x0, matrix products: 289 us -> none  [the longest x1 143 us: channel_mix(): jnp.einsum('bsc,cf->bsf', normed_two, w_ch1, preferred_element_type=jnp.f...]
    pallas_call x0 -> x1, Pallas kernels: none -> 275 us  [layer_call(): pl.pallas_call(functools.partial(kernel, n), out_shape=jax.ShapeDtypeStru...]
    reduce_scatter x1 -> x0, waiting for transfers between devices: 188 us -> none  [local_layer(): lax.psum_scatter(part_pre, 'sp', scatter_dimension=1, tiled=True)]
    all_gather x1 -> x0, waiting for transfers between devices: 90.6 us -> none  [local_layer(): act_full = lax.all_gather(tok_act, 'sp', axis=1, tiled=True)]
    transpose x1, local copies, waits for them, and re-layouts: 37.9 us -> 1.91 us  [local_layer(): w1_rows.T.reshape(n_dev, d // n_dev, s)]
    convert_element_type x1 -> x0, local copies, waits for them, and re-layouts: 32.6 us -> none  [channel_mix(): return (mid_wide + ch_out).astype(jnp.bfloat16)]
    reduce_sum x3 -> x0, other arithmetic: 31.1 us -> none  [the longest x2 21.4 us: layer_norm(): var_val = jnp.mean(centred * centred, axis=-1, keepdims=True)]
    unnamed x25 -> x2, local copies, waits for them, and re-layouts: 32.8 us -> 22.5 us
  transfers between devices with their start and end apart: 2 -> 0, of which waited for: 2 -> 0; matrix products, arithmetic and copies ran while one was open for 0% -> 0% of each run, Pallas kernels for 0% -> 0%
where the time goes in v2:
time: 311 us; the launch traced here: 308 us
  Pallas kernels  275 us (88%)
  local copies, waits for them, and re-layouts  33.6 us (11%)
    pallas_call x1, Pallas kernels, layer_call(): pl.pallas_call(functools.partial(kernel, n), out_shape=jax.ShapeDtypeStru...  275 us
    unnamed x2, local copies, waits for them, and re-layouts  22.5 us

profile of v2, /device:TPU:113, one launch (start us, length us, event | category | flops | bytes accessed | tf_op | source)
XLA Modules:
  0.0 308.2 jit_solution(9471221817744345400)
XLA Ops:
  0.0 1.3 broadcast_in_dim.27.bc2_ref
  1.3 1.3 broadcast_in_dim.28.gain1_ref
  2.6 1.3 broadcast_in_dim.29.bias1_ref
  3.8 1.3 broadcast_in_dim.30.gain2_ref
  5.1 1.3 broadcast_in_dim.31.bias2_ref
  6.4 1.3 copy.19.b1_ref
  7.7 1.5 copy.20.b2_ref
  9.3 1.9 copy.17
  11.2 2.0 copy.18
  13.1 274.6 %shard_map.127 = bf16[32,512,768]{2,1,0:T(8,128)(2,1)} custom-call(bf16[32,512,768]{2,1,0:T(8,128)(2,1)} %x_hbm.1, bf16[8,48,512]{2,1,0:T(8,128)(2,1)} %bitcast.6, bf16[512,384]{1,0:T(8,128)(2,1)} %bitcast.7, bf16[768,3072]{1,0:T(8,128)(2,1)} %wc1_hbm.1, bf16[3072,768]{1,0:T(8,128)(2,1)} %wc2_hbm.1, f32[48,1]{1,0:T(8,128)} %copy.19.b1_ref, ...), custom_call_target="tpu_custom_call" | custom-call | tf_op jit(solution)/shard_map/pallas_call | solution.py:320
  287.7 20.5 %copy.22 = bf16[32,512,768]{2,1,0:T(8,128)(2,1)} copy(bf16[32,512,768]{2,1,0:T(8,128)(2,1)} %shard_map.127) | data formatting | bytes 50331648

commit v3 on v2

v3 whole, which is shorter than its diff:
```python
import functools

import jax
import jax.numpy as jnp
from jax import lax
from jax.experimental import pallas as pl
from jax.experimental.pallas import tpu as pltpu
from jax.sharding import PartitionSpec as P

LN_EPS = 1e-6
GELU_A = 0.7978845608028654
GELU_B = 0.7978845608028654 * 0.044715
BF, F32 = jnp.bfloat16, jnp.float32
SLOTS = 8
NT1, NT2, LNR, ORDER = 256, 768, 32, 0
TAIL = 2
SEND_PAIR, SUM_PAIR, SEND_FAR, SUM_FAR, SEND_NEAR, SUM_NEAR = 1, 2, 3, 4, 5, 7
SEND_ACT, FORWARD, SHARE, TOKEN, MAIN = 8, 10, 11, 12, 13


def gelu(v):
    inner = v * (GELU_A + GELU_B * (v * v))
    return (0.5 * v) * (1.0 + jnp.tanh(inner))


def layer_norm(values, gain, bias):
    rows, width = values.shape
    mean = jnp.sum(values, axis=-1, keepdims=True) * (1.0 / width)
    centred = values - mean
    var = jnp.sum(centred * centred, axis=-1, keepdims=True) * (1.0 / width)
    out = (centred * lax.rsqrt(var + LN_EPS)).reshape(rows // 8, 8, width) * gain[None] + bias[None]
    return out.reshape(rows, width)


def dot(a, b):
    return lax.dot_general(a, b, (((1,), (0,)), ((), ())), preferred_element_type=F32)


def as_column(row):
    n = row.shape[1]
    same = lax.broadcasted_iota(jnp.int32, (n, n), 0) == lax.broadcasted_iota(jnp.int32, (n, n), 1)
    return jnp.sum(jnp.where(same, jnp.broadcast_to(row, (n, n)), 0.0), axis=1, keepdims=True)


def spread(main, extra):
    done = 0
    for k, fn in enumerate(main):
        fn()
        upto = (len(extra) * (k + 1)) // len(main)
        for g in extra[done:upto]:
            g()
        done = upto


def run(fns):
    for fn in fns:
        fn()


def mlp_steps(abufs, acc, wc1, wc2, bc1, bc2):
    wide, chan = abufs[0].shape[1], acc.shape[1]

    def p1(s, v):
        def piece(c):
            k = s * wide + c
            pre = dot(v[...], wc1[:, k:k + NT1]) + bc1[:, k:k + NT1]
            abufs[s][:, c:c + NT1] = gelu(pre).astype(BF)
        return [functools.partial(piece, c) for c in range(0, wide, NT1)]

    def p2(s, x1=None, z=None):
        def piece(c):
            cols = slice(c, c + NT2)
            out = dot(abufs[s][...], wc2[s * wide:(s + 1) * wide, cols])
            if s == 0:
                acc[:, cols] = out + (x1[:, cols].astype(F32) + bc2[:, cols])
            elif s == 1:
                acc[:, cols] += out
            else:
                z[:, cols] = (acc[:, cols] + out).astype(BF)
        return [functools.partial(piece, c) for c in range(0, chan, NT2)]
    return p1, p2


def kernel(n_img, x_hbm, w1_hbm, w2_hbm, wc1_hbm, wc2_hbm, b1_ref, b2_ref, bc1_ref, *refs):
    vec_refs, (z_hbm, tail_hbm, *refs) = refs[:5], refs[5:]
    (xa, xt, zb, w1raw, w2raw, w1t, w1p, w2t, wc1, wc2, vecs, b1c, b2c, u, own, pair_out, pair_in, q0, q1, far_out, far_in, near_out, near_in, act,
     x1, v, x1b, a0, a1, a2, acc, sem_xa, sem_xt, sem_z, sem_w, sem_t, send_sems, recv_sems) = refs
    rows, chan = x1.shape
    half = chan // 2
    part = act.shape[3]
    n_dev = 2 * act.shape[1]
    me = lax.axis_index("sp")
    core = lax.rem(me, 2)
    sib = me + 1 - 2 * core
    up = lax.rem(me + 2, n_dev)
    down = lax.rem(me + n_dev - 2, n_dev)
    far = lax.rem(me + 4, n_dev)

    def s8(i):
        return lax.rem(i, SLOTS)

    def s4(i):
        return lax.rem(i, 4)

    def remote(kind, i, src, dst, to):
        return pltpu.make_async_remote_copy(
            src_ref=src, dst_ref=dst, send_sem=send_sems.at[kind, s8(i)], recv_sem=recv_sems.at[kind, s8(i)],
            device_id={"sp": to}, device_id_type=pl.DeviceIdType.MESH)

    lo, hi = pl.ds(0, half), pl.ds(half, half)

    def out_pair(i):
        return [remote(0, i, pair_out.at[s4(i)], pair_in.at[s8(i)], sib)]

    def out_far(i):
        return [remote(1, i, far_out.at[s4(i), 0], far_in.at[s8(i), 0], up),
                remote(2, i, far_out.at[s4(i), 1], far_in.at[s8(i), 1], down)]

    def out_near(i):
        return [remote(3, i, near_out.at[s4(i), 0], near_in.at[s8(i), 0], up),
                remote(4, i, near_out.at[s4(i), 1], near_in.at[s8(i), 1], down)]

    def block(i, k):
        return act.at[s8(i), k // 2, lax.rem(k, 2)]

    def out_act(i):
        b = block(i, me)
        return [remote(5, i, b, b, up), remote(6, i, b, b, down)]

    def out_forward(i):
        lower_half, upper_half = block(i, down).at[:, lo], block(i, up).at[:, hi]
        return [remote(7, i, lower_half, lower_half, up), remote(8, i, upper_half, upper_half, down)]

    def out_share(i):
        b = act.at[s8(i), :, core]
        return [remote(9, i, b, b, sib)]

    def in_act(i):
        lower, upper = block(i, down), block(i, up)
        return [remote(5, i, lower, lower, up), remote(6, i, upper, upper, down)]

    def in_forward(i):
        a, b = block(i, far).at[:, lo], block(i, far).at[:, hi]
        return [remote(7, i, a, a, up), remote(8, i, b, b, down)]

    def in_share(i):
        b = act.at[s8(i), :, 1 - core]
        return [remote(9, i, b, b, sib)]

    def load_xa(i):
        return pltpu.make_async_copy(x_hbm.at[i], xa.at[s4(i)], sem_xa.at[s4(i)])

    def load_xt(i):
        return pltpu.make_async_copy(x_hbm.at[i], xt.at[lax.rem(i, 2)], sem_xt.at[lax.rem(i, 2)])

    def store_z(i):
        return pltpu.make_async_copy(zb.at[lax.rem(i, 3)], z_hbm.at[i], sem_z.at[lax.rem(i, 3)])

    load_xa(0).start()
    w_copies = [pltpu.make_async_copy(s, d, sem_w.at[k]) for k, (s, d) in enumerate(
        [(w1_hbm, w1raw), (w2_hbm, w2raw), (wc1_hbm, wc1), (wc2_hbm, wc2)])]
    w_copies[0].start()
    load_xa(1).start()
    load_xa(2).start()
    for c in w_copies[1:]:
        c.start()

    barrier = pltpu.get_barrier_semaphore()
    for peer in (sib, up, down):
        pl.semaphore_signal(barrier, inc=1, device_id={"sp": peer}, device_id_type=pl.DeviceIdType.MESH)
    for k, ref in enumerate(vec_refs):
        vecs[k] = jnp.broadcast_to(ref[...].reshape(1, chan), (8, chan))
    w_copies[0].wait()
    for k in range(n_dev):
        w1t[k] = w1raw[:, k * part:(k + 1) * part].astype(F32).T.astype(BF)
    for r in range(n_dev):
        k = lax.rem(me - core + 2 * (r % 4), n_dev) + (core if r < 4 else 1 - core)
        w1p[r * part:(r + 1) * part, :] = w1t[k]
    pl.semaphore_wait(barrier, 3)
    gain1, bias1, gain2, bias2 = (vecs.at[k] for k in range(4))
    bc2 = vecs.at[4, pl.ds(0, 1)]

    def norm_one(i):
        slot = s4(i)

        def piece(r):
            xs = xa[slot, r:r + LNR, :].astype(F32)
            u[r:r + LNR, :] = layer_norm(xs, gain1[...], bias1[...]).astype(BF)
        return [functools.partial(piece, r) for r in range(0, rows, LNR)]

    def partial(i):
        slot = s4(i)
        for c in range(0, chan, 256):
            p = dot(w1p[...], u[:, c:c + 256])
            for r in range(4):
                own[slot, r, :, c:c + 256] = p[r * part:(r + 1) * part]
                pair_out[slot, r, :, c:c + 256] = p[(4 + r) * part:(5 + r) * part].astype(BF)

    def sum_pair(i):
        slot, big_slot = s4(i), s8(i)
        def total(r):
            return own[slot, r] + pair_in[big_slot, r].astype(F32)
        q0[big_slot] = total(0)
        q1[big_slot, 0] = total(1)
        q1[big_slot, 1] = total(3)
        t = total(2).astype(BF)
        far_out[slot, 0] = t[:, :half]
        far_out[slot, 1] = t[:, half:]

    def sum_far(i):
        slot, big_slot = s4(i), s8(i)
        near_out[slot, 0, :, :half] = (q1[big_slot, 0, :, :half] + far_in[big_slot, 0].astype(F32)).astype(BF)
        near_out[slot, 0, :, half:] = q1[big_slot, 0, :, half:].astype(BF)
        near_out[slot, 1, :, :half] = q1[big_slot, 1, :, :half].astype(BF)
        near_out[slot, 1, :, half:] = (q1[big_slot, 1, :, half:] + far_in[big_slot, 1].astype(F32)).astype(BF)

    def sum_near(i):
        slot = s8(i)
        for c in range(0, chan, 256):
            h = (q0[slot, :, c:c + 256] + near_in[slot, 0, :, c:c + 256].astype(F32)
                 + near_in[slot, 1, :, c:c + 256].astype(F32)) + b1c[...]
            act[slot, me // 2, core, :, c:c + 256] = gelu(h).astype(BF)

    def token_dot(i, dst):
        slot = lax.rem(i, 2)

        def piece(c):
            gv = act[s8(i), :, :, :, c:c + 256].reshape(n_dev * part, 256)
            t = dot(w2t[...], gv) + b2c[...]
            dst[:, c:c + 256] = (xt[slot, :, c:c + 256].astype(F32) + t).astype(BF)
        return [functools.partial(piece, c) for c in range(0, chan, 256)]

    def norm_two(src, dst):
        def piece(r):
            xs = src[r:r + LNR, :].astype(F32)
            dst[r:r + LNR, :] = layer_norm(xs, gain2[...], bias2[...]).astype(BF)
        return [functools.partial(piece, r) for r in range(0, rows, LNR)]

    p1, p2 = mlp_steps((a0, a1, a2), acc, wc1, wc2, bc1_ref, bc2)

    def boundary(t, when):
        def each(i, make, method):
            def run(j):
                for c in make(j):
                    getattr(c, method)()
            when(i, run)

        def sends(lag, make):
            each(t - lag - 2, make, "wait_send")
            each(t - lag, make, "start")

        def arrives(lag, make):
            each(t - lag, make, "wait_recv")

        arrives(SUM_FAR, out_far)
        arrives(SHARE, in_forward)
        arrives(FORWARD, in_act)
        arrives(SUM_NEAR, out_near)
        sends(SEND_FAR, out_far)
        sends(FORWARD, out_forward)
        sends(SEND_NEAR, out_near)
        sends(SEND_ACT, out_act)
        sends(SHARE, out_share)
        sends(SEND_PAIR, out_pair)
        arrives(SUM_PAIR, out_pair)
        arrives(TOKEN, in_share)
        when(t + 1, lambda i: load_xa(i).wait(), edge=True)
        when(t + 3, lambda i: load_xa(i).start(), edge=True)
        when(t - TOKEN, lambda i: load_xt(i).wait())
        when(t - TOKEN + 1, lambda i: load_xt(i).start())
        when(t - MAIN - 4, lambda i: store_z(i).wait(), edge=True)
        when(t - MAIN - 2, lambda i: store_z(i).start(), edge=True)

    def guard(i, fn, edge=True):
        @pl.when(jnp.logical_and(i >= 0, i < n_img))
        def _():
            fn(i)

    load_xa(0).wait()
    run(norm_one(0))

    def start_up(t, _):
        boundary(t, guard)
        guard(t - SUM_NEAR, sum_near)
        guard(t - SUM_FAR, sum_far)
        guard(t - SUM_PAIR, sum_pair)
        partial(t)
        run(norm_one(t + 1))

        @pl.when(t == 1)
        def _():
            w_copies[1].wait()
            w2t[...] = w2raw[...].astype(F32).T.astype(BF)
            b1c[...] = as_column(b1_ref[...])
            for r in range(0, rows, 128):
                b2c[r:r + 128, :] = as_column(b2_ref[:, r:r + 128])

        @pl.when(t == TOKEN)
        def _():
            run(token_dot(t - TOKEN, x1))
        return 0

    lax.fori_loop(0, MAIN, start_up, 0)
    w_copies[2].wait()
    w_copies[3].wait()

    def compute(n, dots, norm, sums):
        spread(p2(2, z=zb.at[lax.rem(n + 2, 3)]), norm_two(x1, v))
        run(p1(0, v))
        run(dots)
        run(p1(1, v))
        spread(p2(0, x1=x1), norm)
        run(p1(2, v))
        spread(p2(1), sums)
        run(token_dot(n + 1, x1))

    def steady(t, _):
        boundary(t, lambda i, fn, edge=False: guard(i, fn) if edge else fn(i))
        compute(t - MAIN, [lambda: partial(t)], norm_one(t + 1),
                [lambda: sum_pair(t - SUM_PAIR), lambda: sum_far(t - SUM_FAR),
                 lambda: sum_near(t - SUM_NEAR)])
        return 0

    lax.fori_loop(MAIN, n_img, steady, 0)

    def drain(t, _):
        boundary(t, guard)
        guard(t - SUM_PAIR, sum_pair)
        guard(t - SUM_FAR, sum_far)
        guard(t - SUM_NEAR, sum_near)
        compute(t - MAIN, [], [], [])
        return 0

    end = n_img - TAIL + MAIN
    lax.fori_loop(n_img, end, drain, 0)

    def tail(k, src):
        return pltpu.make_async_copy(src, tail_hbm.at[k], sem_t.at[k])

    tail(0, x1).start()
    boundary(end, guard)
    spread(p2(2, z=zb.at[(end - MAIN + 2) % 3]), norm_two(x1, v))
    tail(1, v).start()
    run(token_dot(n_img - 1, x1b))
    run(norm_two(x1b, u))
    tail(2, x1b).start()
    tail(3, u).start()
    boundary(end + 1, guard)
    for i in (end - MAIN - 2, end - MAIN - 1):
        store_z(i).wait()
    for k, src in enumerate((x1, v, x1b, u)):
        tail(k, src).wait()


def tail_kernel(z_main, tail_hbm, wc1_hbm, wc2_hbm, bc1_ref, bc2_ref, z_hbm,
                ring, tail, zb, wc1, wc2, bc2, a0, a1, a2, acc, sem_in, sem_out, sem_t, sem_w, sem_z):
    n_main = z_main.shape[0]
    wide = a0.shape[1]
    tails = [pltpu.make_async_copy(tail_hbm.at[k], tail.at[k], sem_t.at[k]) for k in (1, 0, 3, 2)]
    w_up = [pltpu.make_async_copy(wc1_hbm.at[:, pl.ds(k * wide, wide)], wc1.at[:, pl.ds(k * wide, wide)], sem_w.at[k])
            for k in range(3)]
    w_down = [pltpu.make_async_copy(wc2_hbm.at[pl.ds(k * wide, wide)], wc2.at[pl.ds(k * wide, wide)], sem_w.at[3 + k])
              for k in range(3)]
    loads = [pltpu.make_async_copy(z_main.at[i], ring.at[i], sem_in.at[i]) for i in range(n_main)]
    stores = [pltpu.make_async_copy(ring.at[i], z_hbm.at[i], sem_out.at[i]) for i in range(n_main)]
    for c in [tails[0], w_up[0], w_up[1], tails[1], w_down[0], w_up[2], w_down[1], w_down[2], *tails[2:]] + loads:
        c.start()
    bc2[...] = bc2_ref[...].reshape(1, acc.shape[1])
    p1, p2 = mlp_steps((a0, a1, a2), acc, wc1, wc2, bc1_ref, bc2)
    moved = [0]

    def move(count):
        for i in range(moved[0], min(n_main, moved[0] + count)):
            loads[i].wait()
            stores[i].start()
        moved[0] = min(n_main, moved[0] + count)

    share = -(-n_main // (6 * TAIL - 2))
    for k in range(TAIL):
        x1, v = tail.at[2 * k], tail.at[2 * k + 1]
        first = k == 0
        steps = [([w_up[0], tails[0]], p1(0, v)), ([w_up[1]], p1(1, v)), ([w_down[0], tails[1]], p2(0, x1=x1)),
                 ([w_up[2]], p1(2, v)), ([w_down[1]], p2(1)), ([w_down[2]], p2(2, z=zb.at[k]))]
        if k == 1:
            for c in tails[2:]:
                c.wait()
        for j, (needs, fns) in enumerate(steps):
            if first:
                for c in needs:
                    c.wait()
            if k > 0 or j > 1:
                move(share)
            run(fns)
        pltpu.make_async_copy(zb.at[k], z_hbm.at[n_main + k], sem_z.at[k]).start()
    move(n_main)
    for c in stores:
        c.wait()
    for k in range(TAIL):
        pltpu.make_async_copy(zb.at[k], z_hbm.at[n_main + k], sem_z.at[k]).wait()


def layer_call(x, w1, w2, wc1, wc2, b1, b2, bc1, vectors):
    n, s, c = x.shape
    d = w1.shape[1]
    part = b1.shape[1]
    n_dev = d // part
    f = wc1.shape[1]
    any_spec = pl.BlockSpec(memory_space=pl.ANY)
    vm = pl.BlockSpec(memory_space=pltpu.VMEM)
    half = c // 2
    dma = pltpu.SemaphoreType.DMA
    hidden = [pltpu.VMEM((s, f // 3), BF)] * 3 + [pltpu.VMEM((s, c), F32)]
    z_main, tail = pl.pallas_call(
        functools.partial(kernel, n),
        out_shape=(jax.ShapeDtypeStruct((n - TAIL, s, c), BF), jax.ShapeDtypeStruct((2 * TAIL, s, c), BF)),
        in_specs=[any_spec] * 5 + [vm] * 8,
        out_specs=(any_spec, any_spec),
        scratch_shapes=[
            pltpu.VMEM((4, s, c), BF), pltpu.VMEM((2, s, c), BF), pltpu.VMEM((3, s, c), BF),
            pltpu.VMEM((s, d), BF), pltpu.VMEM((d, s), BF), pltpu.VMEM((n_dev, part, s), BF),
            pltpu.VMEM((d, s), BF), pltpu.VMEM((s, d), BF), pltpu.VMEM((c, f), BF), pltpu.VMEM((f, c), BF),
            pltpu.VMEM((5, 8, c), F32), pltpu.VMEM((part, 1), F32), pltpu.VMEM((s, 1), F32),
            pltpu.VMEM((s, c), BF),
            pltpu.VMEM((4, 4, part, c), F32), pltpu.VMEM((4, 4, part, c), BF), pltpu.VMEM((SLOTS, 4, part, c), BF),
            pltpu.VMEM((SLOTS, part, c), F32), pltpu.VMEM((SLOTS, 2, part, c), F32),
            pltpu.VMEM((4, 2, part, half), BF), pltpu.VMEM((SLOTS, 2, part, half), BF),
            pltpu.VMEM((4, 2, part, c), BF), pltpu.VMEM((SLOTS, 2, part, c), BF),
            pltpu.VMEM((SLOTS, n_dev // 2, 2, part, c), BF),
            pltpu.VMEM((s, c), BF), pltpu.VMEM((s, c), BF), pltpu.VMEM((s, c), BF), *hidden,
            dma((4,)), dma((2,)), dma((3,)), dma((4,)), dma((4,)), dma((10, SLOTS)), dma((10, SLOTS)),
        ],
        compiler_params=pltpu.CompilerParams(vmem_limit_bytes=62 * 1024 * 1024, collective_id=0, has_side_effects=True),
        name="mixer",
    )(x, w1, w2, wc1, wc2, b1, b2, bc1, *vectors)
    return pl.pallas_call(
        tail_kernel,
        out_shape=jax.ShapeDtypeStruct((n, s, c), BF),
        in_specs=[any_spec] * 4 + [vm] * 2,
        out_specs=any_spec,
        scratch_shapes=[
            pltpu.VMEM((n - TAIL, s, c), BF), pltpu.VMEM((2 * TAIL, s, c), BF), pltpu.VMEM((TAIL, s, c), BF),
            pltpu.VMEM((c, f), BF), pltpu.VMEM((f, c), BF), pltpu.VMEM((1, c), F32), *hidden,
            dma((n - TAIL,)), dma((n - TAIL,)), dma((2 * TAIL,)), dma((6,)), dma((TAIL,)),
        ],
        compiler_params=pltpu.CompilerParams(vmem_limit_bytes=62 * 1024 * 1024),
        name="tail",
    )(z_main, tail, wc1, wc2, bc1, vectors[4])


def solution(mesh):
    row_spec = P("dp", "sp", None)

    def local_layer(x_blk, w1_rows, b1_part, w2_cols, b2_part, w_ch1, b_ch1, w_ch2, b_ch2, ln1_gain, ln1_bias, ln2_gain, ln2_bias):
        return layer_call(x_blk, w1_rows, w2_cols, w_ch1, w_ch2, b1_part[None], b2_part[None], b_ch1[None],
                          (ln1_gain, ln1_bias, ln2_gain, ln2_bias, b_ch2))

    in_specs = (row_spec, P("sp", None), P("sp"), P(None, "sp"), P("sp"), P(None, None), P(None), P(None, None), P(None), P(None), P(None), P(None), P(None))
    return jax.shard_map(local_layer, mesh=mesh, in_specs=in_specs, out_specs=row_spec, check_vma=False)
```

time: 311 us -> 284 us (0.913)
  local copies, waits for them, and re-layouts: 33.6 us -> 0 us
  Pallas kernels: 275 us -> 281 us
    unnamed x2 -> x0, local copies, waits for them, and re-layouts: 22.5 us -> none
    broadcast_in_dim x7 -> x0, local copies, waits for them, and re-layouts: 9.25 us -> none  [the longest x1 1.54 us: local_layer(): b2_part[:, None]]
    pallas_call x1 -> x2, Pallas kernels: 275 us -> 281 us  [the longest x1 255 us: layer_call(): pl.pallas_call(functools.partial(kernel, n), out_shape=(jax.ShapeDtypeStr...]
where the time goes in v3:
time: 284 us; the launch traced here: 281 us
  Pallas kernels  281 us (99%)
    pallas_call x1, Pallas kernels, layer_call(): pl.pallas_call(functools.partial(kernel, n), out_shape=(jax.ShapeDtypeStr...  255 us
    pallas_call x1, Pallas kernels, layer_call(): pl.pallas_call(tail_kernel, out_shape=jax.ShapeDtypeStruct((n, s, c), BF)...  26.3 us

profile of v3, /device:TPU:113, one launch (start us, length us, event | category | flops | bytes accessed | tf_op | source)
XLA Modules:
  0.0 281.2 jit_solution(12892346285120383359)
XLA Ops:
  0.0 254.7 %mixer.1 = (bf16[30,512,768]{2,1,0:T(8,128)(2,1)}, bf16[4,512,768]{2,1,0:T(8,128)(2,1)}) custom-call(bf16[32,512,768]{2,1,0:T(8,128)(2,1)} %x_hbm.1, bf16[512,384]{1,0:T(8,128)(2,1)} %w1_hbm.1, bf16[384,512]{1,0:T(8,128)(2,1)} %w2_hbm.1, bf16[768,3072]{1,0:T(8,128)(2,1)} %wc1_hbm.3, bf16[3072,768]{1,0:T(8,128)(2,1)} %wc2_hbm.3, f32[1,48]{1,0:T(1,128)} %bitcast.6, ...), custom_call_target="tpu_custom_call" | custom-call | tf_op jit(solution)/shard_map/mixer/pallas_call | solution.py:413
  254.7 26.3 %tail.1 = bf16[32,512,768]{2,1,0:T(8,128)(2,1)} custom-call(bf16[30,512,768]{2,1,0:T(8,128)(2,1)} %get-tuple-element.7.z_main, bf16[4,512,768]{2,1,0:T(8,128)(2,1)} %get-tuple-element.8.tail_hbm, bf16[768,3072]{1,0:T(8,128)(2,1)} %wc1_hbm.3, bf16[3072,768]{1,0:T(8,128)(2,1)} %wc2_hbm.3, f32[1,3072]{1,0:T(1,128)} %bitcast.4, f32[768]{0:T(1024)} %bc2_ref.1), custom_call_target="tpu_custom_call" | custom-call | tf_op jit(solution)/shard_map/tail/pallas_call | solution.py:435
